TPU v7x, 32 devices: a whole 2x2x4 slice. The times are simulated.
32 devices in a mesh: pass: 4 (over y, x), red: 4 (over z), grp: 2 (over core).
Axes of the slice: x: 2, y: 2, z: 4, core: 2. Of those that a mesh axis runs over, the one named last changes fastest.
Arguments:
- query_lex: bfloat16 [1536, 16384], P(None, 'red')
- query_dense: bfloat16 [1536, 4096], P(None, 'red')
- passage_lex: bfloat16 [4096, 16384], P(('pass', 'grp'), 'red'), may hold values from 0 to 0.47
- passage_dense: bfloat16 [4096, 4096], P(('pass', 'grp'), 'red'), may hold values from -1.33 to 1.33
- positives: int32 [1536], replicated, may hold values from 0 to 4095
Outputs:
- loss_rows: float32 [1536], P('red')
- grad_query_lex: float32 [1536, 16384], P(('pass', 'grp'), 'red')
- grad_query_dense: float32 [1536, 4096], P(('pass', 'grp'), 'red')
- grad_passage_lex: float32 [4096, 16384], P(('pass', 'grp'), 'red')
- grad_passage_dense: float32 [4096, 4096], P(('pass', 'grp'), 'red')
All inputs are finite; a program needn't handle non-finite values.
Results may differ from a plain program's by a relative error of at most 0.0022.
Values may be sent and summed in bfloat16 or wider, within the bound.
A program may use at most 192 MiB of HBM per device.

v0:
```python
import jax
import jax.numpy as jnp
from jax import lax
from jax.sharding import PartitionSpec as P


def contract_rows(first, second):
    return lax.dot_general(
        first, second, (((1,), (1,)), ((), ())), preferred_element_type=jnp.float32
    )


def contract_columns(first, second):
    return lax.dot_general(
        first, second, (((0,), (0,)), ((), ())), preferred_element_type=jnp.float32
    )


def on_device(query_lex, query_dense, passage_lex, passage_dense, positives):
    lex_partial = contract_rows(query_lex, passage_lex)
    dense_partial = contract_rows(query_dense, passage_dense)
    red_count = lax.axis_size("red")
    red_place = lax.axis_index("red")
    own_queries = query_lex.shape[0] // red_count
    local_passages = passage_lex.shape[0]
    first_column = lax.axis_index(("pass", "grp")) * local_passages
    lexical, dense_logit = (
        lax.psum_scatter(lex_partial, "red", scatter_dimension=0, tiled=True),
        lax.psum_scatter(dense_partial, "red", scatter_dimension=0, tiled=True),
    )
    first_query = red_place * own_queries
    query_count = lexical.shape[0]
    targets = lax.dynamic_slice_in_dim(positives, first_query, query_count)
    columns = first_column + lax.broadcasted_iota(jnp.int32, (1, local_passages), 1)
    target_mask = (targets[:, None] == columns).astype(jnp.float32)
    joined_logit = dense_logit + 0.3 * lexical
    scores = (joined_logit, dense_logit, lexical)
    picked = tuple((jnp.sum(target_mask * logits, axis=1) for logits in scores))
    maxima = lax.pmax(tuple((jnp.max(logits, axis=1) for logits in scores)), ("pass", "grp"))
    powers = tuple((jnp.exp(scores[slot] - maxima[slot][:, None]) for slot in range(3)))
    gathered = lax.psum(
        (
            jnp.sum(powers[0], axis=1),
            jnp.sum(powers[1], axis=1),
            jnp.sum(powers[2], axis=1),
            jnp.sum(powers[0] * (joined_logit - dense_logit), axis=1),
            jnp.sum(powers[0] * (joined_logit - lexical), axis=1),
        )
        + picked,
        ("pass", "grp"),
    )
    totals = gathered[0:3]
    weighted = gathered[3:5]
    picked_all = gathered[5:8]
    log_totals = tuple((maxima[slot] + jnp.log(totals[slot]) for slot in range(3)))
    probability = tuple((jnp.exp(scores[slot] - log_totals[slot][:, None]) for slot in range(3)))
    kl_dense = weighted[0] / totals[0] - log_totals[0] + log_totals[1]
    kl_lex = weighted[1] / totals[0] - log_totals[0] + log_totals[2]
    loss_rows = (
        log_totals[0]
        - picked_all[0]
        + 0.5 * (log_totals[1] - picked_all[1])
        + 0.5 * (log_totals[2] - picked_all[2])
        + 0.5 * kl_dense
        + 0.5 * kl_lex
    )
    grad_dense = (0.5 * probability[0] + probability[1] - 1.5 * target_mask).astype(jnp.bfloat16)
    grad_lex = (-0.2 * probability[0] + probability[2] - 0.8 * target_mask).astype(jnp.bfloat16)
    grad_dense, grad_lex = (
        lax.all_gather(grad_dense, "red", axis=0, tiled=True),
        lax.all_gather(grad_lex, "red", axis=0, tiled=True),
    )
    grad_passage_lex = contract_columns(grad_lex, query_lex)
    grad_passage_dense = contract_columns(grad_dense, query_dense)
    combined = lax.psum_scatter(
        jnp.concatenate(
            [
                jnp.dot(grad_lex, passage_lex, preferred_element_type=jnp.float32),
                jnp.dot(grad_dense, passage_dense, preferred_element_type=jnp.float32),
            ],
            axis=1,
        ),
        ("pass", "grp"),
        scatter_dimension=0,
        tiled=True,
    )
    lex_columns = passage_lex.shape[1]
    return (
        loss_rows,
        combined[:, :lex_columns],
        combined[:, lex_columns:],
        grad_passage_lex,
        grad_passage_dense,
    )


def solution(mesh):
    return jax.shard_map(
        on_device,
        mesh=mesh,
        in_specs=(
            P(None, "red"),
            P(None, "red"),
            P(("pass", "grp"), "red"),
            P(("pass", "grp"), "red"),
            P(),
        ),
        out_specs=(
            P("red"),
            P(("pass", "grp"), "red"),
            P(("pass", "grp"), "red"),
            P(("pass", "grp"), "red"),
            P(("pass", "grp"), "red"),
        ),
        check_vma=False,
    )
```

profile of v0, /device:TPU:0, one launch (start us, length us, event | category | flops | bytes accessed | tf_op | source)
XLA Modules:
  0.0 494.3 jit_solution(13504890629669928803)
XLA Ops:
  7.2 1.8 copy-done
  9.1 4.7 fusion.10
  13.9 12.1 %fusion.11 = f32[1536,512]{1,0:T(8,128)} fusion(bf16[1536,4096]{1,0:T(8,128)(2,1)} %param.5, bf16[512,4096]{1,0:T(8,128)(2,1)} %param.7), kind=kOutput, calls=%fused_computation.29 | convolution fusion | flops 6442450944 | bytes 19922944 | tf_op jit(solution)/shard_map/dot_general | solution.py:8
  26.0 0.8 dynamic_slice.3
  26.8 50.3 %reduce-scatter.4.cloned.1.call-done = f32[384,512]{1,0:T(8,128)} async-done(((f32[1536,512]{1,0:T(8,128)}), f32[384,512]{1,0:T(8,128)}) %reduce-scatter.4.cloned.1.call-update) | async-done | bytes 786448 | tf_op jit(solution)/shard_map/reduce_scatter | solution.py:29
  77.1 63.2 %reduce-scatter.6.cloned.1.call-done = f32[384,512]{1,0:T(8,128)} async-done(((f32[1536,512]{1,0:T(8,128)}), f32[384,512]{1,0:T(8,128)}) %reduce-scatter.6.cloned.1.call-update) | async-done | bytes 786448 | tf_op jit(solution)/shard_map/reduce_scatter | solution.py:28
  140.3 1.6 fusion.9
  141.9 13.4 %all-reduce.1 = (f32[384]{0:T(512)S(1)}, f32[384]{0:T(512)S(1)}, f32[384]{0:T(512)S(1)}) all-reduce(f32[384]{0:T(512)S(1)} %get-tuple-element.15, f32[384]{0:T(512)S(1)} %get-tuple-element.14, f32[384]{0:T(512)S(1)} %get-tuple-element.13), channel_id=1, replica_groups=mesh['pass'=4,'red'=4,'grp'=2] {'pass','grp'}, use_global_device_ids=true, to_apply=%region_15.0 | all-reduce | flops 1152 | bytes 9216 | tf_op jit(solution)/shard_map/pmax | solution.py:39
  155.4 2.5 multiply_reduce_fusion.1
  157.9 22.3 %all-reduce = (f32[384]{0:T(512)S(1)}, f32[384]{0:T(512)S(1)}, f32[384]{0:T(512)S(1)}, f32[384]{0:T(512)S(1)}, f32[384]{0:T(512)S(1)}, /*index=5*/f32[384]{0:T(512)S(1)}, f32[384]{0:T(512)S(1)}, f32[384]{0:T(512)S(1)}) all-reduce(f32[384]{0:T(512)S(1)} %get-tuple-element.11, ...), channel_id=1, replica_groups=mesh['pass'=4,'red'=4,'grp'=2] {'pass','grp'}, use_global_device_ids=true, to_apply=%region_17.0 | all-reduce | flops 3072 | bytes 24576 | tf_op jit(solution)/shard_map/psum | solution.py:41
  180.2 0.6 multiply_add_fusion.1
  180.8 2.9 fusion.4
  183.7 0.5 all-gather.3.cloned.1.call-update
  184.3 0.2 reduce-scatter.8.cloned.1.call-start
  184.5 34.9 %all-gather.5.cloned.1.call-done = bf16[1536,512]{1,0:T(8,128)(2,1)} async-done(((bf16[384,512]{1,0:T(8,128)(2,1)}), bf16[1536,512]{1,0:T(8,128)(2,1)}) %all-gather.5.cloned.1.call-update) | async-done | bytes 1572880 | tf_op jit(solution)/shard_map/all_gather | solution.py:70
  219.4 6.2 %fusion.13 = f32[1536,1024]{1,0:T(8,128)} fusion(bf16[1536,512]{1,0:T(8,128)(2,1)} %all-gather.5.cloned.1.call-done, bf16[512,1024]{1,0:T(8,128)(2,1)} %param.8), kind=kOutput, calls=%fused_computation.31 | convolution fusion | flops 1610612736 | bytes 8912896 | tf_op jit(solution)/shard_map/dot_general | solution.py:79
  225.6 31.7 %all-gather.3.cloned.1.call-done = bf16[1536,512]{1,0:T(8,128)(2,1)} async-done(((bf16[384,512]{1,0:T(8,128)(2,1)}), bf16[1536,512]{1,0:T(8,128)(2,1)}) %all-gather.3.cloned.1.call-update) | async-done | bytes 1572880 | tf_op jit(solution)/shard_map/all_gather | solution.py:71
  257.3 13.9 %fusion.12 = f32[1536,4096]{1,0:T(8,128)} fusion(bf16[1536,512]{1,0:T(8,128)(2,1)} %all-gather.3.cloned.1.call-done, bf16[512,4096]{1,0:T(8,128)(2,1)} %param.7), kind=kOutput, calls=%fused_computation.30 | convolution fusion | flops 6442450944 | bytes 30932992 | tf_op jit(solution)/shard_map/dot_general | solution.py:78
  271.2 19.8 %pad_maximum_fusion = f32[1536,5120]{1,0:T(8,128)} fusion(f32[1536,1024]{1,0:T(8,128)S(1)} %copy-done.1, f32[1536,4096]{1,0:T(8,128)} %fusion.12), kind=kLoop, calls=%fused_computation | loop fusion | flops 7864320 | bytes 62914560 | tf_op jit(solution)/shard_map/concatenate | solution.py:76
  291.1 4.7 fusion.15
  295.8 12.5 %fusion.14 = f32[512,4096]{1,0:T(8,128)} fusion(bf16[1536,512]{1,0:T(8,128)(2,1)S(1)} %copy-done.2, bf16[1536,4096]{1,0:T(8,128)(2,1)} %param.5), kind=kOutput, calls=%fused_computation.32 | convolution fusion | flops 6442450944 | bytes 22544384 | tf_op jit(solution)/shard_map/dot_general | solution.py:14
  308.3 173.5 %reduce-scatter.8.cloned.1.call-done = f32[192,5120]{1,0:T(8,128)} async-done(((f32[1536,5120]{1,0:T(8,128)}), f32[192,5120]{1,0:T(8,128)}) %reduce-scatter.8.cloned.1.call-update) | async-done | bytes 3932176 | tf_op jit(solution)/shard_map/reduce_scatter | solution.py:75
  481.8 3.9 slice.8
  485.7 2.1 slice.9
  (14 shorter events, 0.2 us)
Async XLA Ops:
  7.2 1.9 copy-start
  7.2 69.9 %reduce-scatter.4.cloned.1.call-start = ((), (), s32[]{:S(2)}) async-start(), calls=%async_computation.3 | async-start | bytes 3932160 | tf_op jit(solution)/shard_map/reduce_scatter | solution.py:29
  13.8 126.5 %reduce-scatter.6.cloned.1.call-start = ((), (), s32[]{:S(2)}) async-start(), calls=%async_computation.4 | async-start | bytes 3932160 | tf_op jit(solution)/shard_map/reduce_scatter | solution.py:28
  25.9 193.5 %all-gather.5.cloned.1.call-start = ((), (), s32[]{:S(2)}) async-start(), calls=%async_computation.6 | async-start | bytes 1966080 | tf_op jit(solution)/shard_map/all_gather | solution.py:70
  183.7 73.6 %all-gather.3.cloned.1.call-start = ((), (), s32[]{:S(2)}) async-start(), calls=%async_computation.5 | async-start | bytes 1966080 | tf_op jit(solution)/shard_map/all_gather | solution.py:71
  184.3 297.6 %reduce-scatter.8.cloned.1.call-start = ((), (), s32[]{:S(2)}) async-start(), calls=%async_computation.7 | async-start | bytes 35389440 | tf_op jit(solution)/shard_map/reduce_scatter | solution.py:75
  257.3 13.9 %copy-start.1 = (f32[1536,1024]{1,0:T(8,128)S(1)}, f32[1536,1024]{1,0:T(8,128)}, u32[]{:S(2)}) copy-start(f32[1536,1024]{1,0:T(8,128)} %fusion.13) | copy-start | bytes 18874372
  291.1 4.7 copy-start.2
Sparse Core Ops, SparseCore 0:
  13.9 63.1 reduce-scatter.3
  80.0 60.2 reduce-scatter.5
  183.8 35.5 all-gather.4
  221.4 35.8 all-gather.2
  291.2 190.5 reduce-scatter.7
where the time goes:
time: 495 us; the launch traced here: 494 us
  waiting for transfers between devices  354 us (72%)
  matrix products  54.1 us (11%)
  blocking collectives  35.8 us (7%)
  other arithmetic  27.4 us (6%)
  between operations  13.8 us (3%)
  local copies, waits for them, and re-layouts  8.57 us (2%)
    reduce_scatter x1, waiting for transfers between devices, on_device(): lax.psum_scatter(jnp.concatenate([jnp.dot(grad_lex, passage_lex, preferre...  174 us
    reduce_scatter x1, waiting for transfers between devices, on_device(): lax.psum_scatter(lex_partial, 'red', scatter_dimension=0, tiled=True)  63.2 us
    reduce_scatter x1, waiting for transfers between devices, on_device(): lax.psum_scatter(dense_partial, 'red', scatter_dimension=0, tiled=True)  50.3 us
    all_gather x1, waiting for transfers between devices, on_device(): lax.all_gather(grad_dense, 'red', axis=0, tiled=True)  34.9 us
    all_gather x1, waiting for transfers between devices, on_device(): lax.all_gather(grad_lex, 'red', axis=0, tiled=True)  31.7 us
    psum x1, blocking collectives, on_device(): lax.psum((jnp.sum(powers[0], axis=1), jnp.sum(powers[1], axis=1), jnp.sum...  22.3 us
    concatenate x1, other arithmetic, on_device(): jnp.concatenate([jnp.dot(grad_lex, passage_lex, preferred_element_type=jn...  19.8 us
    dot_general x2, matrix products, contract_columns(): lax.dot_general(first, second, (((0,), (0,)), ((), ())), preferred_elemen...  17.2 us
  transfers between devices with their start and end apart: 5, of which 5 were waited for; matrix products, arithmetic and copies ran while one was open for 7% of the time, Pallas kernels for 0%

commit v1 on v0

--- a/solution.py
+++ b/solution.py
@@ -16,7 +16,21 @@
     )
 
 
+def turn(count, step):
+    return [(i, (i + step) % count) for i in range(count)]
+
+
+def from_chip(rows):
+    count = lax.axis_size("grp")
+    pieces = [rows]
+    for step in range(1, count):
+        pieces.append(lax.ppermute(rows, "grp", turn(count, step)))
+    return jnp.concatenate(pieces, axis=0)
+
+
 def on_device(query_lex, query_dense, passage_lex, passage_dense, positives):
+    chip_passage_lex = from_chip(passage_lex)
+    chip_passage_dense = from_chip(passage_dense)
     lex_partial = contract_rows(query_lex, passage_lex)
     dense_partial = contract_rows(query_dense, passage_dense)
     red_count = lax.axis_size("red")
@@ -35,23 +49,23 @@
     target_mask = (targets[:, None] == columns).astype(jnp.float32)
     joined_logit = dense_logit + 0.3 * lexical
     scores = (joined_logit, dense_logit, lexical)
-    picked = tuple((jnp.sum(target_mask * logits, axis=1) for logits in scores))
-    maxima = lax.pmax(tuple((jnp.max(logits, axis=1) for logits in scores)), ("pass", "grp"))
-    powers = tuple((jnp.exp(scores[slot] - maxima[slot][:, None]) for slot in range(3)))
-    gathered = lax.psum(
-        (
-            jnp.sum(powers[0], axis=1),
-            jnp.sum(powers[1], axis=1),
-            jnp.sum(powers[2], axis=1),
+    local_max = tuple((jnp.max(logits, axis=1) for logits in scores))
+    powers = tuple((jnp.exp(scores[slot] - local_max[slot][:, None]) for slot in range(3)))
+    stats = jnp.stack(
+        local_max
+        + tuple((jnp.sum(power, axis=1) for power in powers))
+        + (
             jnp.sum(powers[0] * (joined_logit - dense_logit), axis=1),
             jnp.sum(powers[0] * (joined_logit - lexical), axis=1),
         )
-        + picked,
-        ("pass", "grp"),
+        + tuple((jnp.sum(target_mask * logits, axis=1) for logits in scores))
     )
-    totals = gathered[0:3]
-    weighted = gathered[3:5]
-    picked_all = gathered[5:8]
+    everyone = lax.all_gather(stats, ("pass", "grp"), axis=0)
+    maxima = jnp.max(everyone[:, 0:3], axis=0)
+    factors = jnp.exp(everyone[:, 0:3] - maxima)
+    totals = jnp.sum(factors * everyone[:, 3:6], axis=0)
+    weighted = jnp.sum(factors[:, 0:1] * everyone[:, 6:8], axis=0)
+    picked_all = jnp.sum(everyone[:, 8:11], axis=0)
     log_totals = tuple((maxima[slot] + jnp.log(totals[slot]) for slot in range(3)))
     probability = tuple((jnp.exp(scores[slot] - log_totals[slot][:, None]) for slot in range(3)))
     kl_dense = weighted[0] / totals[0] - log_totals[0] + log_totals[1]
@@ -70,25 +84,73 @@
         lax.all_gather(grad_dense, "red", axis=0, tiled=True),
         lax.all_gather(grad_lex, "red", axis=0, tiled=True),
     )
+    pass_count = lax.axis_size("pass")
+    pass_place = lax.axis_index("pass")
+    grp_count = lax.axis_size("grp")
+    grp_place = lax.axis_index("grp")
+    block = query_lex.shape[0] // (pass_count * grp_count)
+
+    def for_core(grads, core):
+        blocks = grads.reshape(pass_count, grp_count, block, grads.shape[1])
+        return lax.dynamic_index_in_dim(blocks, core, 1, keepdims=False)
+
+    def with_chip(grads):
+        pieces = [for_core(grads, grp_place)]
+        for step in range(1, grp_count):
+            away = for_core(grads, lax.rem(grp_place + step, grp_count))
+            pieces.append(lax.ppermute(away, "grp", turn(grp_count, step)))
+        return jnp.concatenate(pieces, axis=2)
+
+    chip_lex = with_chip(grad_lex)
+    chip_dense = with_chip(grad_dense)
+
+    def query_terms(place):
+        return (
+            jnp.dot(
+                lax.dynamic_index_in_dim(chip_lex, place, 0, keepdims=False),
+                chip_passage_lex,
+                preferred_element_type=jnp.float32,
+            ),
+            jnp.dot(
+                lax.dynamic_index_in_dim(chip_dense, place, 0, keepdims=False),
+                chip_passage_dense,
+                preferred_element_type=jnp.float32,
+            ),
+        )
+
+    power_of_two = pass_count & (pass_count - 1) == 0
+    leaving = []
+    for step in reversed(range(1, pass_count)):
+        place = (
+            lax.bitwise_xor(pass_place, step)
+            if power_of_two
+            else lax.rem(pass_place + step, pass_count)
+        )
+        perm = (
+            [(i, i ^ step) for i in range(pass_count)]
+            if power_of_two
+            else [(i, (i + step) % pass_count) for i in range(pass_count)]
+        )
+        terms = tuple(term.astype(jnp.bfloat16) for term in query_terms(place))
+        leaving.append((terms, perm))
+    sent = tuple(terms for terms, _ in leaving)
+    sent, grad_lex, grad_dense, chip_lex, chip_dense = lax.optimization_barrier(
+        (sent, grad_lex, grad_dense, chip_lex, chip_dense)
+    )
+    arrived = [
+        tuple(lax.ppermute(term, "pass", perm) for term in terms)
+        for terms, (_, perm) in zip(sent, leaving)
+    ]
     grad_passage_lex = contract_columns(grad_lex, query_lex)
     grad_passage_dense = contract_columns(grad_dense, query_dense)
-    combined = lax.psum_scatter(
-        jnp.concatenate(
-            [
-                jnp.dot(grad_lex, passage_lex, preferred_element_type=jnp.float32),
-                jnp.dot(grad_dense, passage_dense, preferred_element_type=jnp.float32),
-            ],
-            axis=1,
-        ),
-        ("pass", "grp"),
-        scatter_dimension=0,
-        tiled=True,
-    )
-    lex_columns = passage_lex.shape[1]
+    grad_query_lex, grad_query_dense = query_terms(pass_place)
+    for term_lex, term_dense in arrived:
+        grad_query_lex = grad_query_lex + term_lex.astype(jnp.float32)
+        grad_query_dense = grad_query_dense + term_dense.astype(jnp.float32)
     return (
         loss_rows,
-        combined[:, :lex_columns],
-        combined[:, lex_columns:],
+        grad_query_lex,
+        grad_query_dense,
         grad_passage_lex,
         grad_passage_dense,
     )

time: 495 us -> 362 us (0.73)
  waiting for transfers between devices: 354 us -> 243 us
  blocking collectives: 35.8 us -> 9.23 us
  other arithmetic: 27.4 us -> 9.25 us
  local copies, waits for them, and re-layouts: 8.57 us -> 19.1 us
  starting transfers between devices: 0.38 us -> 10.3 us
    reduce_scatter x1 -> x0, waiting for transfers between devices: 174 us -> none  [on_device(): lax.psum_scatter(jnp.concatenate([jnp.dot(grad_lex, passage_lex, preferre...]
    ppermute x0 -> x10, waiting for transfers between devices: none -> 66.7 us  [the longest x6 66.7 us: on_device(): lax.ppermute(term, 'pass', perm)]
    psum x1 -> x0, blocking collectives: 22.3 us -> none  [on_device(): lax.psum((jnp.sum(powers[0], axis=1), jnp.sum(powers[1], axis=1), jnp.sum...]
    concatenate x1 -> x2, other arithmetic: 19.8 us -> 1.53 us  [with_chip(): return jnp.concatenate(pieces, axis=2)]
    pmax x1 -> x0, blocking collectives: 13.4 us -> none  [on_device(): lax.pmax(tuple((jnp.max(logits, axis=1) for logits in scores)), ('pass',...]
    reduce_scatter x1, waiting for transfers between devices: 50.3 us -> 63.2 us  [on_device(): lax.psum_scatter(dense_partial, 'red', scatter_dimension=0, tiled=True)]
    ppermute x0 -> x10, starting transfers between devices: none -> 9.92 us  [the longest x6 8.88 us: on_device(): lax.ppermute(term, 'pass', perm)]
    all_gather x0 -> x1, blocking collectives: none -> 9.23 us  [on_device(): everyone = lax.all_gather(stats, ('pass', 'grp'), axis=0)]
  transfers between devices with their start and end apart: 5 -> 14, of which waited for: 5 -> 6; matrix products, arithmetic and copies ran while one was open for 7% -> 16% of each run, Pallas kernels for 0% -> 0%
where the time goes in v1:
time: 362 us; the launch traced here: 361 us
  waiting for transfers between devices  243 us (67%)
  matrix products  56.6 us (16%)
  local copies, waits for them, and re-layouts  19.1 us (5%)
  between operations  14.1 us (4%)
  starting transfers between devices  10.3 us (3%)
  other arithmetic  9.25 us (3%)
  blocking collectives  9.23 us (3%)
    ppermute x6, waiting for transfers between devices, on_device(): lax.ppermute(term, 'pass', perm)  66.7 us
    reduce_scatter x1, waiting for transfers between devices, on_device(): lax.psum_scatter(dense_partial, 'red', scatter_dimension=0, tiled=True)  63.2 us
    reduce_scatter x1, waiting for transfers between devices, on_device(): lax.psum_scatter(lex_partial, 'red', scatter_dimension=0, tiled=True)  57.1 us
    all_gather x1, waiting for transfers between devices, on_device(): lax.all_gather(grad_dense, 'red', axis=0, tiled=True)  29.4 us
    all_gather x1, waiting for transfers between devices, on_device(): lax.all_gather(grad_lex, 'red', axis=0, tiled=True)  26 us
    dot_general x2, matrix products, contract_rows(): lax.dot_general(first, second, (((1,), (1,)), ((), ())), preferred_elemen...  16.9 us
    dot_general x4, matrix products, query_terms(): jnp.dot(lax.dynamic_index_in_dim(chip_lex, place, 0, keepdims=False), chi...  15 us
    dot_general x2, matrix products, contract_columns(): lax.dot_general(first, second, (((0,), (0,)), ((), ())), preferred_elemen...  14.9 us
  transfers between devices with their start and end apart: 14, of which 6 were waited for; matrix products, arithmetic and copies ran while one was open for 16% of the time, Pallas kernels for 0%

profile of v1, /device:TPU:0, one launch (start us, length us, event | category | flops | bytes accessed | tf_op | source)
XLA Modules:
  0.0 361.3 jit_solution(1406312510967911010)
XLA Ops:
  7.2 12.2 %fusion.60 = f32[1536,512]{1,0:T(8,128)} fusion(bf16[1536,4096]{1,0:T(8,128)(2,1)} %param.5, bf16[512,4096]{1,0:T(8,128)(2,1)} %param.7), kind=kOutput, calls=%fused_computation.112 | convolution fusion | flops 6442450944 | bytes 19922944 | tf_op jit(solution)/shard_map/dot_general | solution.py:8
  19.5 4.7 %fusion.59 = f32[1536,512]{1,0:T(8,128)} fusion(bf16[1536,1024]{1,0:T(8,128)(2,1)S(1)} %copy-done, bf16[512,1024]{1,0:T(8,128)(2,1)} %param.8), kind=kOutput, calls=%fused_computation.111 | convolution fusion | flops 1610612736 | bytes 7340032 | tf_op jit(solution)/shard_map/dot_general | solution.py:8
  25.6 57.1 %reduce-scatter.5.cloned.1.call-done = f32[384,512]{1,0:T(8,128)} async-done(((f32[1536,512]{1,0:T(8,128)}), f32[384,512]{1,0:T(8,128)}) %reduce-scatter.5.cloned.1.call-update) | async-done | bytes 786448 | tf_op jit(solution)/shard_map/reduce_scatter | solution.py:42
  82.7 63.2 %reduce-scatter.3.cloned.1.call-done = f32[384,512]{1,0:T(8,128)} async-done(((f32[1536,512]{1,0:T(8,128)}), f32[384,512]{1,0:T(8,128)}) %reduce-scatter.3.cloned.1.call-update) | async-done | bytes 786448 | tf_op jit(solution)/shard_map/reduce_scatter | solution.py:43
  147.6 2.5 multiply_reduce_fusion
  150.2 9.2 %all-gather.1 = f32[8,11,384]{2,1,0:T(8,128)S(1)} all-gather(f32[1,11,384]{2,1,0:T(8,128)S(1)} %bitcast.58), channel_id=2, replica_groups=mesh['pass'=4,'red'=4,'grp'=2] {'pass','grp'}, dimensions={0}, use_global_device_ids=true | all-gather | bytes 152064 | tf_op jit(solution)/shard_map/all_gather | solution.py:63
  159.6 2.9 fusion.10
  163.5 2.3 constant_dynamic-update-slice_fusion.3
  165.8 4.7 %constant_dynamic-update-slice_fusion.1 = bf16[1024,4096]{1,0:T(8,128)(2,1)} fusion(bf16[512,4096]{1,0:T(8,128)(2,1)} %param.7), kind=kLoop, calls=%fused_computation.75 | loop fusion | bytes 8388608
  170.5 2.3 constant_dynamic-update-slice_fusion.2
  172.8 26.0 %all-gather.5.cloned.1.call-done = bf16[1536,512]{1,0:T(8,128)(2,1)} async-done(((bf16[384,512]{1,0:T(8,128)(2,1)}), bf16[1536,512]{1,0:T(8,128)(2,1)}) %all-gather.5.cloned.1.call-update) | async-done | bytes 1572880 | tf_op jit(solution)/shard_map/all_gather | solution.py:85
  198.7 2.6 dynamic-slice_bitcast_fusion.2
  201.3 4.7 %constant_dynamic-update-slice_fusion = bf16[1024,4096]{1,0:T(8,128)(2,1)} fusion(bf16[1024,4096]{1,0:T(8,128)(2,1)} %constant_dynamic-update-slice_fusion.1, bf16[512,4096]{1,0:T(8,128)(2,1)} %collective-permute-done.1), kind=kLoop, calls=%fused_computation.74 | loop fusion | bytes 8388608 | tf_op jit(solution)/shard_map/concatenate | solution.py:28
  206.6 29.4 %all-gather.7.cloned.1.call-done = bf16[1536,512]{1,0:T(8,128)(2,1)} async-done(((bf16[384,512]{1,0:T(8,128)(2,1)}), bf16[1536,512]{1,0:T(8,128)(2,1)}) %all-gather.7.cloned.1.call-update) | async-done | bytes 1572880 | tf_op jit(solution)/shard_map/all_gather | solution.py:84
  237.9 5.5 %convolution_convert_fusion.2 = bf16[192,4096]{1,0:T(8,128)(2,1)S(1)} fusion(bf16[1024,4096]{1,0:T(8,128)(2,1)} %constant_dynamic-update-slice_fusion, s32[]{:T(128)S(6)} %select_n.32, bf16[4,192,512]{2,1,0:T(8,128)(2,1)S(1)} %copy-done.1, bf16[4,192,512]{2,1,0:T(8,128)(2,1)} %collective-permute-done), kind=kOutput, calls=%fused_computation.5 | convolution fusion | flops 1612185600 | bytes 11534340 | tf_op jit(solution)/shard_map/dot_general | solution.py:109
  243.3 2.8 convolution_convert_fusion.1
  250.5 2.8 convolution_convert_fusion
  263.5 11.8 %fusion.61 = f32[512,4096]{1,0:T(8,128)} fusion(bf16[1536,512]{1,0:T(8,128)(2,1)S(1)} %copy-done.2, bf16[1536,4096]{1,0:T(8,128)(2,1)} %param.5), kind=kOutput, calls=%fused_computation.113 | convolution fusion | flops 6442450944 | bytes 22544384 | tf_op jit(solution)/shard_map/dot_general | solution.py:14
  275.2 60.7 %collective-permute-done.9 = bf16[192,1024]{1,0:T(8,128)(2,1)S(1)} collective-permute-done((bf16[192,1024]{1,0:T(8,128)(2,1)S(1)}, bf16[192,1024]{1,0:T(8,128)(2,1)S(1)}, u32[]{:S(2)}, u32[]{:S(2)}) %collective-permute-start.9) | collective-permute-done | bytes 393248 | tf_op jit(solution)/shard_map/ppermute | solution.py:141
  336.0 2.4 collective-permute-start.7
  338.4 3.1 fusion.62
  341.5 6.0 %collective-permute-done.7 = bf16[192,1024]{1,0:T(8,128)(2,1)S(1)} collective-permute-done((bf16[192,1024]{1,0:T(8,128)(2,1)S(1)}, bf16[192,1024]{1,0:T(8,128)(2,1)S(1)}, u32[]{:S(2)}, u32[]{:S(2)}) %collective-permute-start.7) | collective-permute-done | bytes 393248 | tf_op jit(solution)/shard_map/ppermute | solution.py:141
  347.5 3.2 fusion.3
  350.7 4.1 %fusion.1 = f32[192,4096]{1,0:T(8,128)} fusion(bf16[1024,4096]{1,0:T(8,128)(2,1)S(1)} %bitcast.55, bf16[192,4096]{1,0:T(8,128)(2,1)S(1)} %collective-permute-done.6, bf16[192,4096]{1,0:T(8,128)(2,1)S(1)} %collective-permute-done.5, bf16[192,4096]{1,0:T(8,128)(2,1)S(1)} %collective-permute-done.4, bf16[4,192,1024]{2,1,0:T(8,128)(2,1)S(1)} %pad_maximum_fusion, ...), kind=kOutput, calls=%fused_computation.2 | convolution fusion | flops 1615331328 | bytes 16646148 | tf_op jit(solution)/shard_map/dot_general | solution.py:109
  (66 shorter events, 21.3 us)
Async XLA Ops:
  7.2 12.3 %copy-start = (bf16[1536,1024]{1,0:T(8,128)(2,1)S(1)}, bf16[1536,1024]{1,0:T(8,128)(2,1)}, u32[]{:S(2)}) copy-start(bf16[1536,1024]{1,0:T(8,128)(2,1)} %param.6) | copy-start | bytes 9437188
  7.2 75.6 %reduce-scatter.5.cloned.1.call-start = ((), (), s32[]{:S(2)}) async-start(), calls=%async_computation.3 | async-start | bytes 3932160 | tf_op jit(solution)/shard_map/reduce_scatter | solution.py:42
  19.4 126.5 %reduce-scatter.3.cloned.1.call-start = ((), (), s32[]{:S(2)}) async-start(), calls=%async_computation.2 | async-start | bytes 3932160 | tf_op jit(solution)/shard_map/reduce_scatter | solution.py:43
  24.3 174.4 %all-gather.5.cloned.1.call-start = ((), (), s32[]{:S(2)}) async-start(), calls=%async_computation.4 | async-start | bytes 1966080 | tf_op jit(solution)/shard_map/all_gather | solution.py:85
  24.3 177.0 %collective-permute-start.1 = (bf16[512,4096]{1,0:T(8,128)(2,1)}, bf16[512,4096]{1,0:T(8,128)(2,1)}, u32[]{:S(2)}, u32[]{:S(2)}) collective-permute-start(bf16[512,4096]{1,0:T(8,128)(2,1)} %param.7), channel_id=1, source_target_pairs={{0,1},{1,0},{2,3},{3,2},{4,5},{5,4},{6,7},{7,6},{8,9},{9,8},{10,11... | collective-permute-start | bytes 12582920 | tf_op jit(solution)/shard_map/ppermute | solution.py:27
  162.5 73.5 %all-gather.7.cloned.1.call-start = ((), (), s32[]{:S(2)}) async-start(), calls=%async_computation.5 | async-start | bytes 1966080 | tf_op jit(solution)/shard_map/all_gather | solution.py:84
  163.1 7.4 %collective-permute-start.3 = (bf16[512,1024]{1,0:T(8,128)(2,1)}, bf16[512,1024]{1,0:T(8,128)(2,1)}, u32[]{:S(2)}, u32[]{:S(2)}) collective-permute-start(bf16[512,1024]{1,0:T(8,128)(2,1)} %param.8), channel_id=1, source_target_pairs={{0,1},{1,0},{2,3},{3,2},{4,5},{5,4},{6,7},{7,6},{8,9},{9,8},{10,11... | collective-permute-start | bytes 3145736 | tf_op jit(solution)/shard_map/ppermute | solution.py:27
  201.3 36.5 %collective-permute-start = (bf16[4,192,512]{2,1,0:T(8,128)(2,1)}, bf16[4,192,512]{2,1,0:T(8,128)(2,1)}, u32[]{:S(2)}, u32[]{:S(2)}) collective-permute-start(bf16[4,192,512]{2,1,0:T(8,128)(2,1)} %get-tuple-element.54), channel_id=1, source_target_pairs={{0,1},{1,0},{2,3},{3,2},{4,5},{5,4},{6,7},{7,6},{8,9},{9,8},{10,11... | collective-permute-start | bytes 2359304 | tf_op jit(solution)/shard_map/ppermute | solution.py:101
  236.1 1.8 copy-start.1
  236.1 7.3 %slice-start = ((s8[8388608]{0:T(1024)(128)(4,1)}), s8[4194304]{0:T(1024)(128)(4,1)S(1)}, s32[]{:S(2)}) async-start(s8[8388608]{0:T(1024)(128)(4,1)} %bitcast.54), calls=%async_computation.6 | async-start | bytes 8388608
  237.7 8.4 %collective-permute-start.2 = (bf16[4,192,512]{2,1,0:T(8,128)(2,1)S(1)}, bf16[4,192,512]{2,1,0:T(8,128)(2,1)S(1)}, u32[]{:S(2)}, u32[]{:S(2)}) collective-permute-start(bf16[4,192,512]{2,1,0:T(8,128)(2,1)S(1)} %get-tuple-element.52), channel_id=1, source_target_pairs={{0,1},{1,0},{2,3},{3,2},{4,5},{5,4},{6,7},{7,6},{8,9},{9,8},{10,11... | collective-permute-start | bytes 2359304 | tf_op jit(solution)/shard_map/ppermute | solution.py:101
  237.8 5.5 %slice-start.1 = ((s8[8388608]{0:T(1024)(128)(4,1)}), s8[4194304]{0:T(1024)(128)(4,1)S(1)}, s32[]{:S(2)}) async-start(s8[8388608]{0:T(1024)(128)(4,1)} %bitcast.54), calls=%async_computation.7 | async-start | bytes 8388608
  256.8 6.7 %copy-start.2 = (bf16[1536,512]{1,0:T(8,128)(2,1)S(1)}, bf16[1536,512]{1,0:T(8,128)(2,1)}, u32[]{:S(2)}) copy-start(bf16[1536,512]{1,0:T(8,128)(2,1)} %all-gather.5.cloned.1.call-done) | copy-start | bytes 4718596
  257.0 81.4 %copy-start.3 = (bf16[1536,512]{1,0:T(8,128)(2,1)S(1)}, bf16[1536,512]{1,0:T(8,128)(2,1)}, u32[]{:S(2)}) copy-start(bf16[1536,512]{1,0:T(8,128)(2,1)} %all-gather.7.cloned.1.call-done) | copy-start | bytes 4718596
  257.0 93.7 %collective-permute-start.6 = (bf16[192,4096]{1,0:T(8,128)(2,1)S(1)}, bf16[192,4096]{1,0:T(8,128)(2,1)S(1)}, u32[]{:S(2)}, u32[]{:S(2)}) collective-permute-start(bf16[192,4096]{1,0:T(8,128)(2,1)S(1)} %convolution_convert_fusion), channel_id=1, source_target_pairs={{0,8},{8,0},{16,24},{24,16},{1,9},{9,1},{17,25},{25,17},{2,10},{10... | collective-permute-start | bytes 4718600 | tf_op jit(solution)/shard_map/ppermute | solution.py:141
  258.5 92.2 %collective-permute-start.5 = (bf16[192,4096]{1,0:T(8,128)(2,1)S(1)}, bf16[192,4096]{1,0:T(8,128)(2,1)S(1)}, u32[]{:S(2)}, u32[]{:S(2)}) collective-permute-start(bf16[192,4096]{1,0:T(8,128)(2,1)S(1)} %convolution_convert_fusion.1), channel_id=1, source_target_pairs={{0,16},{8,24},{16,0},{24,8},{1,17},{9,25},{17,1},{25,9},{2,18},{10... | collective-permute-start | bytes 4718600 | tf_op jit(solution)/shard_map/ppermute | solution.py:141
  260.0 90.7 %collective-permute-start.4 = (bf16[192,4096]{1,0:T(8,128)(2,1)S(1)}, bf16[192,4096]{1,0:T(8,128)(2,1)S(1)}, u32[]{:S(2)}, u32[]{:S(2)}) collective-permute-start(bf16[192,4096]{1,0:T(8,128)(2,1)S(1)} %convolution_convert_fusion.2), channel_id=1, source_target_pairs={{0,24},{8,16},{16,8},{24,0},{1,25},{9,17},{17,9},{25,1},{2,26},{10... | collective-permute-start | bytes 4718600 | tf_op jit(solution)/shard_map/ppermute | solution.py:141
  260.5 75.4 %collective-permute-start.9 = (bf16[192,1024]{1,0:T(8,128)(2,1)S(1)}, bf16[192,1024]{1,0:T(8,128)(2,1)S(1)}, u32[]{:S(2)}, u32[]{:S(2)}) collective-permute-start(bf16[192,1024]{1,0:T(8,128)(2,1)S(1)} %convolution_convert_fusion.3), channel_id=1, source_target_pairs={{0,8},{8,0},{16,24},{24,16},{1,9},{9,1},{17,25},{25,17},{2,10},{10... | collective-permute-start | bytes 1179656 | tf_op jit(solution)/shard_map/ppermute | solution.py:141
  262.0 79.5 %collective-permute-start.8 = (bf16[192,1024]{1,0:T(8,128)(2,1)S(1)}, bf16[192,1024]{1,0:T(8,128)(2,1)S(1)}, u32[]{:S(2)}, u32[]{:S(2)}) collective-permute-start(bf16[192,1024]{1,0:T(8,128)(2,1)S(1)} %convolution_convert_fusion.4), channel_id=1, source_target_pairs={{0,16},{8,24},{16,0},{24,8},{1,17},{9,25},{17,1},{25,9},{2,18},{10... | collective-permute-start | bytes 1179656 | tf_op jit(solution)/shard_map/ppermute | solution.py:141
  336.0 11.5 %collective-permute-start.7 = (bf16[192,1024]{1,0:T(8,128)(2,1)S(1)}, bf16[192,1024]{1,0:T(8,128)(2,1)S(1)}, u32[]{:S(2)}, u32[]{:S(2)}) collective-permute-start(bf16[192,1024]{1,0:T(8,128)(2,1)S(1)} %convolution_convert_fusion.5), channel_id=1, source_target_pairs={{0,24},{8,16},{16,8},{24,0},{1,25},{9,17},{17,9},{25,1},{2,26},{10... | collective-permute-start | bytes 1179656 | tf_op jit(solution)/shard_map/ppermute | solution.py:141
Sparse Core Ops, SparseCore 0:
  19.6 63.1 reduce-scatter.4
  85.6 60.2 reduce-scatter.2
  162.6 36.0 all-gather.4
  200.1 35.8 all-gather.6
